TPU v7x, 32 devices: a whole 2x2x4 slice. The times are simulated.
32 devices in a mesh: group: 8 (over z, core), member: 4 (over y, x).
Axes of the slice: x: 2, y: 2, z: 4, core: 2. Of those that a mesh axis runs over, the one named last changes fastest.
Arguments:
- rhs: bfloat16 [8, 4, 768, 128], P('group', 'member'), may hold values from -6 to 6
- leaf_pivot_inverse: bfloat16 [8, 4, 768, 768], P('group', 'member'), may hold values from -1.5 to 1.5, as said below
- leaf_border_block: bfloat16 [8, 4, 512, 768], P('group', 'member'), may hold values from -0.21875 to 0.21875
- leaf_map: int32 [8, 4, 4], P('group'), may hold values from 0 to 47, as said below
- mid_inverse: bfloat16 [8, 2048, 2048], P('group', 'member'), may hold values from -1.5 to 1.5, as said below
- mid_border: bfloat16 [8, 4096, 2048], P('group', None, 'member'), may hold values from -0.125 to 0.125
- root_map: int32 [8, 4, 8], P('group', 'member'), may hold values from 0 to 15, as said below
- root_inverse: bfloat16 [8192, 8192], P('group', 'member'), may hold values from -0.5 to 0.5, as said below
Outputs:
- leaf_solution: bfloat16 [8, 4, 768, 128], P('group', 'member')
- mid_solution: bfloat16 [8, 2048, 128], P('group', 'member')
- root_solution: bfloat16 [4, 2048, 128], P('member', 'group')
Inputs may be any that keep to these rules, and one draw needn't show every extreme that they name: `leaf_map`: for each (g, m) the 4 entries are distinct; a value k below 16 names pivot block k of the mid-level front, a larger one border block k - 16. `root_map`: for each (g, m) the entries are distinct. `leaf_pivot_inverse`: each [768, 768] matrix is lower triangular with a positive diagonal, as the inverse of a Cholesky factor is: every entry above the diagonal is zero. `mid_inverse`: each [2048, 2048] matrix is lower triangular with a positive diagonal, as the inverse of a Cholesky factor is: every entry above the diagonal is zero. `root_inverse`: lower triangular with a positive diagonal, as the inverse of a Cholesky factor is: every entry above the diagonal is zero.
All inputs are finite; a program needn't handle non-finite values.
Results may differ from a plain program's by a relative error of at most 0.028.
Values may be sent and summed in bfloat16 or wider, within the bound.
No kernel may reach another device: no remote copies, remote signals or barrier semaphores. Data moves between devices by JAX's collectives and lax.ppermute only.
A program may use at most 64 MiB of HBM per device.

v0:
```python
import jax
import jax.numpy as jnp
from jax import lax
from jax.sharding import PartitionSpec as P

BLOCK = 128


def assemble(block_ids, targets, source_terms):
    selection_mask = (block_ids[:, None] == targets[None, :]).astype(jnp.bfloat16)
    return jnp.einsum(
        "ng,gcy->ncy", selection_mask, source_terms, preferred_element_type=jnp.float32
    )


def transposed(matrix, values):
    return lax.dot_general(
        matrix, values, (((0,), (0,)), ((), ())), preferred_element_type=jnp.float32
    )


def on_device(
    rhs,
    leaf_pivot_inverse,
    leaf_border_block,
    leaf_map,
    mid_inverse,
    mid_border,
    root_map,
    root_inverse,
):
    members = lax.axis_size("member")
    member = lax.axis_index("member")
    leaf_source = rhs[0, 0]
    leaf_cholesky_factor = leaf_pivot_inverse[0, 0]
    leaf_edge = leaf_border_block[0, 0]
    columns = leaf_source.shape[1]
    leaf_blocks = leaf_edge.shape[0] // BLOCK
    own_pivots = mid_inverse.shape[1]
    pivots = mid_inverse.shape[2]
    border_rows = mid_border.shape[1]
    pivot_blocks = pivots // BLOCK
    front_blocks = pivot_blocks + border_rows // BLOCK
    own_border = border_rows // members
    per_member = own_border // BLOCK
    group_maps = leaf_map[0]
    own_targets = lax.dynamic_index_in_dim(group_maps, member, 0, keepdims=False)
    pivot_ids = jnp.arange(pivot_blocks, dtype=jnp.int32)
    mid_factor = mid_inverse[0]
    mid_edge = mid_border[0]
    leaf_forward_solve = jnp.dot(
        leaf_cholesky_factor, leaf_source, preferred_element_type=jnp.float32
    ).astype(jnp.bfloat16)
    leaf_output = (
        -jnp.dot(leaf_edge, leaf_forward_solve, preferred_element_type=jnp.float32)
    ).astype(jnp.bfloat16)
    gathered = lax.all_gather(
        leaf_output.reshape(1, leaf_blocks, BLOCK, columns), "member", axis=0, tiled=True
    )
    source_terms = gathered.reshape(members * leaf_blocks, BLOCK, columns)
    targets = group_maps.reshape(members * leaf_blocks)
    mid_rhs = (
        assemble(pivot_ids, targets, source_terms).reshape(pivots, columns).astype(jnp.bfloat16)
    )
    border_ids = pivot_blocks + member * per_member + jnp.arange(per_member, dtype=jnp.int32)
    leaf_part = assemble(border_ids, targets, source_terms).reshape(own_border, columns)
    mid_forward = jnp.dot(mid_factor, mid_rhs, preferred_element_type=jnp.float32).astype(
        jnp.bfloat16
    )
    partial_update = -jnp.dot(mid_edge, mid_forward, preferred_element_type=jnp.float32)
    mid_update = (
        lax.psum_scatter(
            partial_update.astype(jnp.bfloat16), "member", scatter_dimension=0, tiled=True
        ).astype(jnp.float32)
        + leaf_part
    )
    share_rows = root_inverse.shape[1]
    root_per = share_rows // BLOCK
    chooser = (root_map[0, 0][:, None] == jnp.arange(root_per, dtype=jnp.int32)[None, :]).astype(
        jnp.float32
    )
    root_term = jnp.einsum(
        "iq,ix->qx",
        chooser,
        mid_update.reshape(per_member, BLOCK * columns),
        precision=lax.Precision.HIGHEST,
    )
    root_rhs = (
        lax.psum(root_term.astype(jnp.bfloat16), "group")
        .astype(jnp.float32)
        .reshape(share_rows, columns)
        .astype(jnp.bfloat16)
    )
    root_part = jnp.dot(root_inverse, root_rhs, preferred_element_type=jnp.float32)
    root_forward = lax.psum(root_part.astype(jnp.bfloat16), "member")
    back_part = transposed(root_inverse, root_forward)
    root_values = lax.psum(back_part.astype(jnp.bfloat16), "group")
    rows_out = share_rows // lax.axis_size("group")
    root_out = lax.dynamic_slice_in_dim(
        root_values, lax.axis_index("group") * rows_out, rows_out, 0
    )[None]
    own_values = jnp.einsum(
        "iq,qx->ix",
        chooser.astype(jnp.bfloat16),
        root_values.reshape(root_per, BLOCK * columns),
        preferred_element_type=jnp.float32,
    )
    own_values = own_values.astype(jnp.bfloat16).reshape(own_border, columns)
    border_values = lax.all_gather(own_values, "member", axis=0, tiled=True)
    mid_back = (mid_forward.astype(jnp.float32) - transposed(mid_edge, border_values)).astype(
        jnp.bfloat16
    )
    mid_part = transposed(mid_factor, mid_back)
    mid_values = lax.psum(mid_part.astype(jnp.bfloat16), "member")
    mid_out = lax.dynamic_slice_in_dim(mid_values, member * own_pivots, own_pivots, 0)[None]
    front_values = jnp.concatenate([mid_values, border_values], axis=0).reshape(
        front_blocks, BLOCK, columns
    )
    all_blocks = jnp.arange(front_blocks, dtype=jnp.int32)
    selected_items = (
        assemble(own_targets, all_blocks, front_values)
        .astype(jnp.bfloat16)
        .reshape(leaf_edge.shape[0], columns)
    )
    leaf_backward_solve = (
        leaf_forward_solve.astype(jnp.float32) - transposed(leaf_edge, selected_items)
    ).astype(jnp.bfloat16)
    leaf_value_rows = transposed(leaf_cholesky_factor, leaf_backward_solve).astype(jnp.bfloat16)
    return (leaf_value_rows[None, None], mid_out, root_out)


def solution(mesh):
    in_specs = (
        P("group", "member", None, None),
        P("group", "member", None, None),
        P("group", "member", None, None),
        P("group", None, None),
        P("group", "member", None),
        P("group", None, "member"),
        P("group", "member", None),
        P("group", "member"),
    )
    out_specs = (
        P("group", "member", None, None),
        P("group", "member", None),
        P("member", "group", None),
    )
    return jax.shard_map(
        on_device, mesh=mesh, in_specs=in_specs, out_specs=out_specs, check_vma=False
    )
```

profile of v0, /device:TPU:0, one launch (start us, length us, event | category | flops | bytes accessed | tf_op | source)
XLA Modules:
  0.0 320.4 jit_solution(14530798952716888823)
XLA Ops:
  7.2 0.0 reduce-scatter.2.cloned.1.call-start
  7.2 0.9 eq.63
  8.1 1.8 fusion.17
  9.9 1.5 fusion.41
  11.4 0.1 copy.42
  11.5 11.5 %all_gather.6 = bf16[4,4,128,128]{3,2,1,0:T(8,128)(2,1)S(1)} all-gather(bf16[1,4,128,128]{3,2,1,0:T(8,128)(2,1)S(1)} %bitcast.105), channel_id=1, replica_groups=mesh['group'=8,'member'=4] {'member'}, dimensions={0}, use_global_device_ids=true | all-gather | bytes 655360 | tf_op jit(solution)/shard_map/all_gather | solution.py:57
  23.1 0.4 copy.27
  23.5 0.3 convolution_convert_fusion.4
  23.8 0.1 copy.28
  23.9 0.8 fusion.32
  24.8 0.9 copy-done.1
  25.7 2.4 fusion.1
  28.1 0.0 all-reduce.5.cloned.1.call-start
  28.2 0.7 copy.39
  29.0 0.3 fusion.53
  29.2 27.3 %reduce-scatter.2.cloned.1.call-done = bf16[1024,128]{0,1:T(8,128)(2,1)} async-done(((bf16[4096,128]{0,1:T(8,128)(2,1)}), bf16[1024,128]{0,1:T(8,128)(2,1)}) %reduce-scatter.2.cloned.1.call-update) | async-done | bytes 262160 | tf_op jit(solution)/shard_map/reduce_scatter | solution.py:72
  56.5 1.1 bitcast_add_fusion
  57.6 0.2 copy.30
  57.8 0.1 reshape.47
  57.9 0.7 convolution_convert_fusion
  58.6 1.0 convert_element_type.103
  59.7 0.0 all-reduce.7.cloned.1.call-start
  59.7 56.6 %all-reduce.5.cloned.1.call-done = bf16[2048,128]{1,0:T(8,128)(2,1)} async-done(((bf16[2048,128]{1,0:T(8,128)(2,1)}), bf16[2048,128]{1,0:T(8,128)(2,1)}) %all-reduce.5.cloned.1.call-update) | async-done | bytes 524304 | tf_op jit(solution)/shard_map/psum | solution.py:89
  116.3 4.6 %fusion.24 = bf16[1024,128]{0,1:T(8,128)(2,1)} fusion(bf16[2048,128]{1,0:T(8,128)(2,1)} %all-reduce.5.cloned.1.call-done, bf16[1024,2048]{1,0:T(8,128)(2,1)} %param.15), kind=kOutput, calls=%fused_computation.29 | convolution fusion | flops 537001984 | bytes 4980736 | tf_op jit(solution)/shard_map/dot_general | solution.py:94
  120.9 0.0 all-reduce.9.cloned.1.call-start
  121.0 42.2 %all-reduce.7.cloned.1.call-done = bf16[1024,128]{0,1:T(8,128)(2,1)} async-done(((bf16[1024,128]{0,1:T(8,128)(2,1)}), bf16[1024,128]{0,1:T(8,128)(2,1)}) %all-reduce.7.cloned.1.call-update) | async-done | bytes 262160 | tf_op jit(solution)/shard_map/psum | solution.py:95
  163.2 3.8 %fusion.5 = bf16[2048,128]{0,1:T(8,128)(2,1)} fusion(bf16[1024,128]{0,1:T(8,128)(2,1)} %all-reduce.7.cloned.1.call-done, bf16[1024,2048]{1,0:T(8,128)(2,1)} %param.15), kind=kOutput, calls=%fused_computation.10 | convolution fusion | flops 537133056 | bytes 4980736 | tf_op jit(solution)/shard_map/dot_general | solution.py:17
  167.0 0.0 all-gather.2.cloned.1.call-start
  167.1 56.6 %all-reduce.9.cloned.1.call-done = bf16[2048,128]{0,1:T(8,128)(2,1)} async-done(((bf16[2048,128]{0,1:T(8,128)(2,1)}), bf16[2048,128]{0,1:T(8,128)(2,1)}) %all-reduce.9.cloned.1.call-update) | async-done | bytes 524304 | tf_op jit(solution)/shard_map/psum | solution.py:97
  223.7 1.3 copy.31
  225.0 0.2 reshape.48
  225.2 0.3 convolution_convert_fusion.1
  225.5 0.8 reshape.49
  226.3 0.0 all-reduce.11.cloned.1.call-start
  226.4 25.7 %all-gather.2.cloned.1.call-done = bf16[4096,128]{1,0:T(8,128)(2,1)} async-done(((bf16[1024,128]{1,0:T(8,128)(2,1)}), bf16[4096,128]{1,0:T(8,128)(2,1)}) %all-gather.2.cloned.1.call-update) | async-done | bytes 1048592 | tf_op jit(solution)/shard_map/all_gather | solution.py:109
  252.0 4.5 %fusion.6 = bf16[2048,128]{0,1:T(8,128)(2,1)} fusion(bf16[1,512,2048]{2,1,0:T(8,128)(2,1)S(1)} %copy-done, bf16[4096,128]{1,0:T(8,128)(2,1)} %all-gather.2.cloned.1.call-done, bf16[1,4096,512]{2,1,0:T(8,128)(2,1)} %param.13, bf16[128,512]{1,0:T(8,128)(2,1)S(1)} %fusion.32), kind=kOutput, calls=%fused_computation.11 | convolution fusion | flops 805765120 | bytes 7995392 | tf_op jit(solution)/shard_map/dot_general | solution.py:17
  256.5 0.7 fusion.63
  257.2 0.8 constant_dynamic-slice_fusion
  258.1 0.7 copy.37
  258.8 43.3 %all-reduce.11.cloned.1.call-done = bf16[2048,128]{0,1:T(8,128)(2,1)} async-done(((bf16[2048,128]{0,1:T(8,128)(2,1)}), bf16[2048,128]{0,1:T(8,128)(2,1)}) %all-reduce.11.cloned.1.call-update) | async-done | bytes 524304 | tf_op jit(solution)/shard_map/psum | solution.py:114
  302.1 2.0 copy.32
  304.1 1.6 pad_maximum_fusion
  305.7 1.0 fusion.35
  306.6 0.7 copy.34
  307.3 2.8 fusion.29
  310.1 1.7 copy.38
  311.8 0.9 constant_dynamic-slice_fusion.1
  312.7 0.8 copy.36
  (14 shorter events, 0.1 us)
Async XLA Ops:
  7.2 16.8 %copy-start = (bf16[1,512,2048]{2,1,0:T(8,128)(2,1)S(1)}, bf16[1,512,2048]{2,1,0:T(8,128)(2,1)}, u32[]{:S(2)}) copy-start(bf16[1,512,2048]{2,1,0:T(8,128)(2,1)} %param.12) | copy-start | bytes 6291460
  7.2 49.4 %reduce-scatter.2.cloned.1.call-start = ((), (), s32[]{:S(2)}) async-start(), calls=%async_computation.1 | async-start | bytes 1310720 | tf_op jit(solution)/shard_map/reduce_scatter | solution.py:72
  23.5 2.2 copy-start.1
  28.1 88.2 %all-reduce.5.cloned.1.call-start = ((), (), s32[]{:S(2)}) async-start(), calls=%async_computation.2 | async-start | bytes 1048576 | tf_op jit(solution)/shard_map/psum | solution.py:89
  29.0 29.0 %copy-start.3 = (s32[1,1,8]{2,1,0:T(1,128)S(1)}, s32[1,1,8]{2,1,0:T(1,128)}, u32[]{:S(2)}) copy-start(s32[1,1,8]{2,1,0:T(1,128)} %param.14) | copy-start | bytes 100
  59.7 103.5 %all-reduce.7.cloned.1.call-start = ((), (), s32[]{:S(2)}) async-start(), calls=%async_computation.3 | async-start | bytes 524288 | tf_op jit(solution)/shard_map/psum | solution.py:95
  120.9 102.7 %all-reduce.9.cloned.1.call-start = ((), (), s32[]{:S(2)}) async-start(), calls=%async_computation.4 | async-start | bytes 1048576 | tf_op jit(solution)/shard_map/psum | solution.py:97
  167.0 85.0 %all-gather.2.cloned.1.call-start = ((), (), s32[]{:S(2)}) async-start(), calls=%async_computation.5 | async-start | bytes 1310720 | tf_op jit(solution)/shard_map/all_gather | solution.py:109
  226.3 75.7 %all-reduce.11.cloned.1.call-start = ((), (), s32[]{:S(2)}) async-start(), calls=%async_computation.6 | async-start | bytes 1048576 | tf_op jit(solution)/shard_map/psum | solution.py:114
  304.1 3.2 copy-start.2
Sparse Core Ops, SparseCore 0:
  28.3 28.2 reduce-scatter.1
  59.8 56.4 all-reduce.4
  121.0 42.0 all-reduce.6
  167.1 56.5 all-reduce.8
  226.5 25.5 all-gather.1
  256.6 45.3 all-reduce.10
where the time goes:
time: 321 us; the launch traced here: 320 us
  waiting for transfers between devices  252 us (79%)
  matrix products  24.6 us (8%)
  local copies, waits for them, and re-layouts  15.3 us (5%)
  between operations  14.3 us (4%)
  blocking collectives  11.5 us (4%)
    psum x1, waiting for transfers between devices, on_device(): root_values = lax.psum(back_part.astype(jnp.bfloat16), 'group')  56.6 us
    psum x1, waiting for transfers between devices, on_device(): lax.psum(root_term.astype(jnp.bfloat16), 'group').astype(jnp.float32)  56.6 us
    psum x1, waiting for transfers between devices, on_device(): mid_values = lax.psum(mid_part.astype(jnp.bfloat16), 'member')  43.3 us
    psum x1, waiting for transfers between devices, on_device(): root_forward = lax.psum(root_part.astype(jnp.bfloat16), 'member')  42.2 us
    reduce_scatter x1, waiting for transfers between devices, on_device(): lax.psum_scatter(partial_update.astype(jnp.bfloat16), 'member', scatter_d...  27.3 us
    all_gather x1, waiting for transfers between devices, on_device(): border_values = lax.all_gather(own_values, 'member', axis=0, tiled=True)  25.7 us
    all_gather x1, blocking collectives, on_device(): lax.all_gather(leaf_output.reshape(1, leaf_blocks, BLOCK, columns), 'memb...  11.5 us
    dot_general x3, matrix products, transposed(): lax.dot_general(matrix, values, (((0,), (0,)), ((), ())), preferred_eleme...  11 us
  transfers between devices with their start and end apart: 6, of which 6 were waited for; matrix products, arithmetic and copies ran while one was open for 1% of the time, Pallas kernels for 0%

commit v1 on v0

--- a/solution.py
+++ b/solution.py
@@ -1,9 +1,29 @@
+import functools
 import jax
 import jax.numpy as jnp
 from jax import lax
 from jax.sharding import PartitionSpec as P
 
 BLOCK = 128
+
+
+def return_all_thing(shard_in, d_out):
+    fan = lax.axis_size("member")
+    latest = [(ix - 1, ix) for ix in range(1, fan)] + [(fan - 1, 0)]
+    found_now = shard_in
+    at = 0
+    by_rank = [found_now]
+    while at < fan - 1:
+        found_now = lax.ppermute(found_now, "member", latest)
+        by_rank += [found_now]
+        at = at + 1
+    arr_out = jnp.concatenate([*reversed(by_rank)], d_out)
+    lower = lax.axis_index("member")
+    new = jnp.roll(arr_out, (lower + 1) * found_now.shape[d_out], d_out)
+    return new
+
+
+advance_layers_all_on_mesh = functools.partial(return_all_thing, d_out=0)
 
 
 def assemble(block_ids, targets, source_terms):
@@ -106,7 +126,7 @@
         preferred_element_type=jnp.float32,
     )
     own_values = own_values.astype(jnp.bfloat16).reshape(own_border, columns)
-    border_values = lax.all_gather(own_values, "member", axis=0, tiled=True)
+    border_values = advance_layers_all_on_mesh(own_values)
     mid_back = (mid_forward.astype(jnp.float32) - transposed(mid_edge, border_values)).astype(
         jnp.bfloat16
     )

time: 321 us -> 315 us (0.981)
  waiting for transfers between devices: 252 us -> 244 us
  starting transfers between devices: 0.25 us -> 3.74 us
    all_gather x1 -> x0, waiting for transfers between devices: 25.7 us -> none  [on_device(): border_values = lax.all_gather(own_values, 'member', axis=0, tiled=True)]
    ppermute x0 -> x3, waiting for transfers between devices: none -> 19.1 us  [return_all_thing(): found_now = lax.ppermute(found_now, 'member', latest)]
    ppermute x0 -> x3, starting transfers between devices: none -> 3.53 us  [return_all_thing(): found_now = lax.ppermute(found_now, 'member', latest)]
  transfers between devices with their start and end apart: 6 -> 8, of which waited for: 6 -> 8; matrix products, arithmetic and copies ran while one was open for 1% -> 1% of each run, Pallas kernels for 0% -> 0%
where the time goes in v1:
time: 315 us
  waiting for transfers between devices  244 us (77%)
  matrix products  24.3 us (8%)
  local copies, waits for them, and re-layouts  14.9 us (5%)
  between operations  14 us (4%)
  blocking collectives  11.5 us (4%)
  starting transfers between devices  3.74 us (1%)
    psum x1, waiting for transfers between devices, on_device(): root_values = lax.psum(back_part.astype(jnp.bfloat16), 'group')  56.6 us
    psum x1, waiting for transfers between devices, on_device(): lax.psum(root_term.astype(jnp.bfloat16), 'group').astype(jnp.float32)  56.6 us
    psum x1, waiting for transfers between devices, on_device(): root_forward = lax.psum(root_part.astype(jnp.bfloat16), 'member')  42.2 us
    psum x1, waiting for transfers between devices, on_device(): mid_values = lax.psum(mid_part.astype(jnp.bfloat16), 'member')  42.1 us
    reduce_scatter x1, waiting for transfers between devices, on_device(): lax.psum_scatter(partial_update.astype(jnp.bfloat16), 'member', scatter_d...  27.3 us
    ppermute x3, waiting for transfers between devices, return_all_thing(): found_now = lax.ppermute(found_now, 'member', latest)  19.1 us
    all_gather x1, blocking collectives, on_device(): lax.all_gather(leaf_output.reshape(1, leaf_blocks, BLOCK, columns), 'memb...  11.5 us
    dot_general x3, matrix products, transposed(): lax.dot_general(matrix, values, (((0,), (0,)), ((), ())), preferred_eleme...  10.7 us
  transfers between devices with their start and end apart: 8, of which 8 were waited for; matrix products, arithmetic and copies ran while one was open for 1% of the time, Pallas kernels for 0%

profile of v1, /device:TPU:0, one launch (start us, length us, event | category | flops | bytes accessed | tf_op | source)
XLA Modules:
  0.0 314.8 jit_solution(14553276124780337236)
XLA Ops:
  7.2 0.9 eq.66
  8.1 1.8 fusion.17
  9.9 1.5 fusion.41
  11.4 0.1 copy.42
  11.5 11.5 %all_gather.3 = bf16[4,4,128,128]{3,2,1,0:T(8,128)(2,1)S(1)} all-gather(bf16[1,4,128,128]{3,2,1,0:T(8,128)(2,1)S(1)} %bitcast.105), channel_id=1, replica_groups=mesh['group'=8,'member'=4] {'member'}, dimensions={0}, use_global_device_ids=true | all-gather | bytes 655360 | tf_op jit(solution)/shard_map/all_gather | solution.py:77
  23.1 0.4 copy.27
  23.5 0.3 convolution_convert_fusion.4
  23.8 0.1 copy.28
  23.9 0.8 fusion.32
  24.8 0.9 copy-done.1
  25.7 2.4 fusion.1
  28.2 0.7 copy.39
  29.0 0.3 fusion.53
  29.2 27.3 %reduce-scatter.2.cloned.1.call-done = bf16[1024,128]{0,1:T(8,128)(2,1)} async-done(((bf16[4096,128]{0,1:T(8,128)(2,1)}), bf16[1024,128]{0,1:T(8,128)(2,1)}) %reduce-scatter.2.cloned.1.call-update) | async-done | bytes 262160 | tf_op jit(solution)/shard_map/reduce_scatter | solution.py:92
  56.5 1.1 bitcast_add_fusion
  57.6 0.2 copy.30
  57.8 0.1 reshape.47
  57.9 0.7 convolution_convert_fusion
  58.6 1.0 convert_element_type.103
  59.7 56.6 %all-reduce.5.cloned.1.call-done = bf16[2048,128]{1,0:T(8,128)(2,1)} async-done(((bf16[2048,128]{1,0:T(8,128)(2,1)}), bf16[2048,128]{1,0:T(8,128)(2,1)}) %all-reduce.5.cloned.1.call-update) | async-done | bytes 524304 | tf_op jit(solution)/shard_map/psum | solution.py:109
  116.3 4.6 %fusion.24 = bf16[1024,128]{0,1:T(8,128)(2,1)} fusion(bf16[2048,128]{1,0:T(8,128)(2,1)} %all-reduce.5.cloned.1.call-done, bf16[1024,2048]{1,0:T(8,128)(2,1)} %param.15), kind=kOutput, calls=%fused_computation.29 | convolution fusion | flops 537001984 | bytes 4980736 | tf_op jit(solution)/shard_map/dot_general | solution.py:114
  121.0 42.2 %all-reduce.7.cloned.1.call-done = bf16[1024,128]{0,1:T(8,128)(2,1)} async-done(((bf16[1024,128]{0,1:T(8,128)(2,1)}), bf16[1024,128]{0,1:T(8,128)(2,1)}) %all-reduce.7.cloned.1.call-update) | async-done | bytes 262160 | tf_op jit(solution)/shard_map/psum | solution.py:115
  163.2 3.8 %fusion.5 = bf16[2048,128]{0,1:T(8,128)(2,1)} fusion(bf16[1024,128]{0,1:T(8,128)(2,1)} %all-reduce.7.cloned.1.call-done, bf16[1024,2048]{1,0:T(8,128)(2,1)} %param.15), kind=kOutput, calls=%fused_computation.10 | convolution fusion | flops 537133056 | bytes 4980736 | tf_op jit(solution)/shard_map/dot_general | solution.py:37
  167.0 56.6 %all-reduce.9.cloned.1.call-done = bf16[2048,128]{0,1:T(8,128)(2,1)} async-done(((bf16[2048,128]{0,1:T(8,128)(2,1)}), bf16[2048,128]{0,1:T(8,128)(2,1)}) %all-reduce.9.cloned.1.call-update) | async-done | bytes 524304 | tf_op jit(solution)/shard_map/psum | solution.py:117
  223.7 1.3 copy.31
  225.0 0.2 reshape.48
  225.2 0.3 convolution_convert_fusion.1
  225.5 0.1 reshape.49
  225.6 1.5 collective-permute-start
  227.1 5.8 %collective-permute-done = bf16[1024,128]{1,0:T(8,128)(2,1)S(1)} collective-permute-done((bf16[1024,128]{1,0:T(8,128)(2,1)S(1)}, bf16[1024,128]{1,0:T(8,128)(2,1)S(1)}, u32[]{:S(2)}, u32[]{:S(2)}) %collective-permute-start) | collective-permute-done | bytes 262176 | tf_op jit(solution)/shard_map/ppermute | solution.py:17
  232.9 1.1 collective-permute-start.1
  234.0 7.0 %collective-permute-done.1 = bf16[1024,128]{1,0:T(8,128)(2,1)S(1)} collective-permute-done((bf16[1024,128]{1,0:T(8,128)(2,1)S(1)}, bf16[1024,128]{1,0:T(8,128)(2,1)S(1)}, u32[]{:S(2)}, u32[]{:S(2)}) %collective-permute-start.1) | collective-permute-done | bytes 262176 | tf_op jit(solution)/shard_map/ppermute | solution.py:17
  241.0 0.9 collective-permute-start.2
  241.9 6.3 %collective-permute-done.2 = bf16[1024,128]{1,0:T(8,128)(2,1)S(1)} collective-permute-done((bf16[1024,128]{1,0:T(8,128)(2,1)S(1)}, bf16[1024,128]{1,0:T(8,128)(2,1)S(1)}, u32[]{:S(2)}, u32[]{:S(2)}) %collective-permute-start.2) | collective-permute-done | bytes 262176 | tf_op jit(solution)/shard_map/ppermute | solution.py:17
  248.6 0.1 constant_dynamic-slice_fusion.2
  248.7 4.2 %fusion.6 = bf16[2048,128]{0,1:T(8,128)(2,1)} fusion(bf16[1,512,2048]{2,1,0:T(8,128)(2,1)S(1)} %copy-done, bf16[4096,128]{1,0:T(8,128)(2,1)S(1)} %constant_dynamic-slice_fusion.2, bf16[1,4096,512]{2,1,0:T(8,128)(2,1)} %param.13, bf16[128,512]{1,0:T(8,128)(2,1)S(1)} %fusion.32), kind=kOutput, calls=%fused_computation.11 | convolution fusion | flops 805765120 | bytes 7995392 | tf_op jit(solution)/shard_map/dot_general | solution.py:37
  252.8 0.7 fusion.63
  253.5 0.8 constant_dynamic-slice_fusion
  254.4 0.7 copy.37
  255.1 42.1 %all-reduce.11.cloned.1.call-done = bf16[2048,128]{0,1:T(8,128)(2,1)} async-done(((bf16[2048,128]{0,1:T(8,128)(2,1)}), bf16[2048,128]{0,1:T(8,128)(2,1)}) %all-reduce.11.cloned.1.call-update) | async-done | bytes 524304 | tf_op jit(solution)/shard_map/psum | solution.py:134
  297.2 2.0 copy.32
  299.3 1.1 pad_maximum_fusion
  300.4 1.0 fusion.35
  301.4 0.7 copy.34
  302.1 2.8 fusion.29
  304.8 1.7 copy.38
  306.6 0.9 constant_dynamic-slice_fusion.1
  307.5 0.8 copy.36
  (26 shorter events, 0.6 us)
Async XLA Ops:
  7.2 16.8 %copy-start = (bf16[1,512,2048]{2,1,0:T(8,128)(2,1)S(1)}, bf16[1,512,2048]{2,1,0:T(8,128)(2,1)}, u32[]{:S(2)}) copy-start(bf16[1,512,2048]{2,1,0:T(8,128)(2,1)} %param.12) | copy-start | bytes 6291460
  7.2 49.4 %reduce-scatter.2.cloned.1.call-start = ((), (), s32[]{:S(2)}) async-start(), calls=%async_computation.1 | async-start | bytes 1310720 | tf_op jit(solution)/shard_map/reduce_scatter | solution.py:92
  23.5 2.2 copy-start.1
  28.1 88.2 %all-reduce.5.cloned.1.call-start = ((), (), s32[]{:S(2)}) async-start(), calls=%async_computation.2 | async-start | bytes 1048576 | tf_op jit(solution)/shard_map/psum | solution.py:109
  29.0 29.0 %copy-start.3 = (s32[1,1,8]{2,1,0:T(1,128)S(1)}, s32[1,1,8]{2,1,0:T(1,128)}, u32[]{:S(2)}) copy-start(s32[1,1,8]{2,1,0:T(1,128)} %param.14) | copy-start | bytes 100
  59.7 103.5 %all-reduce.7.cloned.1.call-start = ((), (), s32[]{:S(2)}) async-start(), calls=%async_computation.3 | async-start | bytes 524288 | tf_op jit(solution)/shard_map/psum | solution.py:115
  120.9 102.7 %all-reduce.9.cloned.1.call-start = ((), (), s32[]{:S(2)}) async-start(), calls=%async_computation.4 | async-start | bytes 1048576 | tf_op jit(solution)/shard_map/psum | solution.py:117
  167.0 130.2 %all-reduce.11.cloned.1.call-start = ((), (), s32[]{:S(2)}) async-start(), calls=%async_computation.5 | async-start | bytes 1048576 | tf_op jit(solution)/shard_map/psum | solution.py:134
  225.6 7.3 %collective-permute-start = (bf16[1024,128]{1,0:T(8,128)(2,1)S(1)}, bf16[1024,128]{1,0:T(8,128)(2,1)S(1)}, u32[]{:S(2)}, u32[]{:S(2)}) collective-permute-start(bf16[1024,128]{1,0:T(8,128)(2,1)S(1)} %reshape.49), channel_id=1, source_target_pairs={{0,1},{1,2},{2,3},{3,0},{4,5},{5,6},{6,7},{7,4},{8,9},{9,10},{10,1... | collective-permute-start | bytes 786440 | tf_op jit(solution)/shard_map/ppermute | solution.py:17
  232.9 8.0 %collective-permute-start.1 = (bf16[1024,128]{1,0:T(8,128)(2,1)S(1)}, bf16[1024,128]{1,0:T(8,128)(2,1)S(1)}, u32[]{:S(2)}, u32[]{:S(2)}) collective-permute-start(bf16[1024,128]{1,0:T(8,128)(2,1)S(1)} %collective-permute-done), channel_id=1, source_target_pairs={{0,1},{1,2},{2,3},{3,0},{4,5},{5,6},{6,7},{7,4},{8,9},{9,10},{10,1... | collective-permute-start | bytes 786440 | tf_op jit(solution)/shard_map/ppermute | solution.py:17
  241.0 7.3 %collective-permute-start.2 = (bf16[1024,128]{1,0:T(8,128)(2,1)S(1)}, bf16[1024,128]{1,0:T(8,128)(2,1)S(1)}, u32[]{:S(2)}, u32[]{:S(2)}) collective-permute-start(bf16[1024,128]{1,0:T(8,128)(2,1)S(1)} %collective-permute-done.1), channel_id=1, source_target_pairs={{0,1},{1,2},{2,3},{3,0},{4,5},{5,6},{6,7},{7,4},{8,9},{9,10},{10,1... | collective-permute-start | bytes 786440 | tf_op jit(solution)/shard_map/ppermute | solution.py:17
  300.4 1.6 copy-start.2
Sparse Core Ops, SparseCore 0:
  28.3 28.2 reduce-scatter.1
  59.8 56.4 all-reduce.4
  121.0 42.0 all-reduce.6
  167.1 56.5 all-reduce.8
  253.0 44.2 all-reduce.10
